TPU v7x, 32 devices: a whole 2x2x4 slice. The times are simulated.
32 devices in a mesh: track: 16 (over z, y, x), cam: 2 (over core).
Axes of the slice: x: 2, y: 2, z: 4, core: 2. Of those that a mesh axis runs over, the one named last changes fastest.
Arguments:
- omega: bfloat16 [32, 9, 4096], P(None, None, ('track', 'cam')), may hold values from -6 to 6
- u_blocks: float32 [9, 9, 4096], P(None, None, ('track', 'cam')), may hold values from -5.4 to 36, as said below
- w_blocks: bfloat16 [9, 3, 16384], P(None, None, ('track', 'cam')), may hold values from -1.796875 to 1.796875
- v_inverse: float32 [3, 3, 4096], P(None, None, ('track', 'cam')), may hold values from -0.6 to 1.5, as said below
- obs_camera: int32 [16384], P(('track', 'cam')), may hold values from 0 to 4095, as said below
- obs_track: int32 [16384], P(('track', 'cam')), may hold values from 0 to 31, as said below
- obs_mask: int32 [16384], P(('track', 'cam')), may hold values from 0 to 1, as said below
Outputs:
- sketch: float32 [32, 9, 4096], P(None, None, ('track', 'cam'))
- basis: float32 [32, 9, 4096], P(None, None, ('track', 'cam'))
- factor: float32 [32, 32], replicated
Inputs may be any that keep to these rules, and one draw needn't show every extreme that they name: `obs_camera`: cameras c * 128 to (c + 1) * 128 - 1 belong to device c (track slower). Among one device's 512 observations, padding included, at most 32 name cameras of any one device, and exactly 32 name those of some device. `obs_track`: in each aligned block of 128 observations, slots 0 to 31 each hold one track of 2 to 4 consecutive observations from the block's start, in rising order; the padding after them carries slot 31. `obs_mask`: 1 on the observations of tracks, 0 on the padding at the end of each block. `u_blocks`: each block is symmetric. `v_inverse`: each block is symmetric positive definite.
All inputs are finite; a program needn't handle non-finite values.
Results may differ from a plain program's by a relative error of at most 0.00095.
Values may be sent and summed in bfloat16 or wider, within the bound.
A program may use at most 64 MiB of HBM per device.

v0:
```python
import jax
import jax.numpy as jnp
from jax import lax
from jax.sharding import PartitionSpec as P

BLK_OBS = 128
TRK_BLK = 32
HIGH = lax.Precision.HIGHEST


def eliminate(gathered, w_blocks, v_inverse, obs_track, obs_mask):
    weights = w_blocks.astype(jnp.float32)
    live_mask = obs_mask.astype(jnp.float32)
    values = gathered.astype(jnp.float32)
    columns = values.shape[1]
    obs_count = values.shape[2]
    blocks = obs_count // BLK_OBS
    projected = (
        jnp.stack(
            [
                sum(
                    (
                        weights[comp_row, comp_col][None, :] * values[comp_row]
                        for comp_row in range(9)
                    )
                )
                for comp_col in range(3)
            ]
        )
        * live_mask
    )
    member = (
        obs_track.reshape(blocks, BLK_OBS)[:, :, None] == jnp.arange(TRK_BLK, dtype=jnp.int32)
    ).astype(jnp.float32)
    summed = jnp.einsum(
        "icbo,bot->icbt", projected.reshape(3, columns, blocks, BLK_OBS), member, precision=HIGH
    ).reshape(3, columns, blocks * TRK_BLK)
    solved = jnp.stack(
        [
            sum(
                (v_inverse[comp_row, comp_col][None, :] * summed[comp_col] for comp_col in range(3))
            )
            for comp_row in range(3)
        ]
    )
    spread = jnp.einsum(
        "icbt,bot->icbo", solved.reshape(3, columns, blocks, TRK_BLK), member, precision=HIGH
    ).reshape(3, columns, obs_count)
    returned = (
        jnp.stack(
            [
                sum(
                    (
                        weights[comp_row, comp_col][None, :] * spread[comp_col]
                        for comp_col in range(3)
                    )
                )
                for comp_row in range(9)
            ]
        )
        * live_mask
    )
    return returned.astype(jnp.bfloat16)


def on_device(omega, u_blocks, w_blocks, v_inverse, obs_camera, obs_track, obs_mask):
    track_count = lax.axis_size("track")
    cam_count = lax.axis_size("cam")
    devices = track_count * cam_count
    columns, params, cam_width = omega.shape
    obs_count = obs_camera.shape[0]
    capacity = max(2, 2 * obs_count // devices)
    buffer_slots = devices * capacity
    owner_index = obs_camera // cam_width
    ordering = jnp.argsort(owner_index, stable=True)
    ranked = owner_index[ordering]
    first_index = jnp.searchsorted(ranked, ranked, side="left")
    placed = ranked * capacity + jnp.arange(obs_count, dtype=jnp.int32) - first_index
    slot_index = jnp.zeros((obs_count,), jnp.int32).at[ordering].set(placed)
    request = (
        jnp.full((buffer_slots,), -1, jnp.int32)
        .at[slot_index]
        .set(obs_camera)
        .reshape(track_count, cam_count, capacity)
    )
    camera_ids = lax.all_to_all(
        lax.all_to_all(request, "track", split_axis=0, concat_axis=0, tiled=True),
        "cam",
        split_axis=1,
        concat_axis=1,
        tiled=True,
    )
    table_start = (lax.axis_index("track") * cam_count + lax.axis_index("cam")) * cam_width
    table_width = omega.shape[2]
    is_live = camera_ids >= 0
    local_ids = jnp.where(is_live, camera_ids - table_start, 0).reshape(-1)
    gathered_rows = jnp.take(omega, local_ids, axis=2)
    outgoing = (
        gathered_rows.reshape(columns, params, track_count, cam_count, capacity)
        .transpose(2, 3, 1, 4, 0)
        .reshape(track_count, cam_count, params, capacity * columns)
    )
    returned = lax.all_to_all(
        lax.all_to_all(outgoing, "track", split_axis=0, concat_axis=0, tiled=True),
        "cam",
        split_axis=1,
        concat_axis=1,
        tiled=True,
    )
    received = (
        returned.reshape(track_count, cam_count, params, capacity, columns)
        .transpose(2, 4, 0, 1, 3)
        .reshape(params, columns, buffer_slots)
    )
    needed = jnp.take(received, slot_index, axis=2)
    contribution = eliminate(needed, w_blocks, v_inverse, obs_track, obs_mask)
    buffer = (
        jnp.zeros((params, columns, buffer_slots), jnp.bfloat16)
        .at[:, :, slot_index]
        .set(contribution)
    )
    packed = (
        buffer.reshape(params, columns, track_count, cam_count, capacity)
        .transpose(2, 3, 0, 4, 1)
        .reshape(track_count, cam_count, params, capacity * columns)
    )
    arrived = lax.all_to_all(
        lax.all_to_all(packed, "track", split_axis=0, concat_axis=0, tiled=True),
        "cam",
        split_axis=1,
        concat_axis=1,
        tiled=True,
    )
    terms = (
        arrived.reshape(track_count, cam_count, params, capacity, columns)
        .transpose(4, 2, 0, 1, 3)
        .reshape(columns, params, buffer_slots)
        .astype(jnp.float32)
    )
    target = jnp.where(is_live, camera_ids - table_start, table_width).reshape(-1)
    incoming = (
        jnp.zeros((columns, params, table_width + 1), jnp.float32)
        .at[:, :, target]
        .add(terms)[:, :, :table_width]
    )
    own_term = jnp.einsum("mnk,jnk->jmk", u_blocks, omega.astype(jnp.float32), precision=HIGH)
    sketch = own_term - incoming
    flat_rows = sketch.reshape(columns, params * cam_width)
    gram_local = jnp.dot(flat_rows, flat_rows.T, precision=HIGH, preferred_element_type=jnp.float32)
    row_total = params * cam_width * devices
    lower_factor = jnp.linalg.cholesky(lax.psum(gram_local, ("track", "cam")) / row_total)
    basis_rows = jax.scipy.linalg.solve_triangular(lower_factor, flat_rows, lower=True).reshape(
        sketch.shape
    )
    return (sketch, basis_rows, lower_factor.T)


def solution(mesh):
    in_specs = (
        P(None, None, ("track", "cam")),
        P(None, None, ("track", "cam")),
        P(None, None, ("track", "cam")),
        P(None, None, ("track", "cam")),
        P(("track", "cam")),
        P(("track", "cam")),
        P(("track", "cam")),
    )
    out_specs = (P(None, None, ("track", "cam")), P(None, None, ("track", "cam")), P())
    return jax.shard_map(
        on_device, mesh=mesh, in_specs=in_specs, out_specs=out_specs, check_vma=False
    )
```

profile of v0, /device:TPU:0, one launch (start us, length us, event | category | flops | bytes accessed | tf_op | source)
XLA Modules:
  0.0 363.9 jit_solution(12495128076649908816)
XLA Ops:
  1.3 3.8 %sort.17 = (s32[512]{0:T(512)}, s32[512]{0:T(512)S(1)}) sort(s32[512]{0:T(512)S(1)} %add_select_fusion, s32[512]{0:T(512)S(1)} %iota.38), dimensions={0}, to_apply=%region_0.1 | sort | flops 4608 | bytes 8192 | tf_op jit(solution)/shard_map/jit(argsort)/sort | solution.py:75
  5.1 3.5 gather_fusion.1
  8.6 35.9 %while.25 = (s32[]{:T(128)}, u32[512]{0:T(512)S(1)}, u32[512]{0:T(512)S(1)}, s32[512]{0:T(512)S(1)}, s32[]{:T(128)}, /*index=5*/s32[]{:T(128)}, s32[]{}) while((s32[]{:T(128)}, u32[512]{0:T(512)S(1)}, u32[512]{0:T(512)S(1)}, s32[512]{0:T(512)S(1)}, s32[]{:T(128)}, /*index=5*/s32[]{:T(128)}, s32[]{}) %tuple.87), condition=%wide.region_2.3_spmd.clone, body=%wide.region_1.2_spmd.clone.sunk | while | flops 10244 | bytes 40037 | solution.py:77
  8.7 3.5 gather_fusion
  12.3 3.5 gather_fusion
  15.9 3.5 gather_fusion
  19.4 3.5 gather_fusion
  23.0 3.5 gather_fusion
  26.6 3.5 gather_fusion
  30.2 3.5 gather_fusion
  33.8 3.5 gather_fusion
  37.4 3.5 gather_fusion
  41.0 3.5 gather_fusion
  44.5 2.4 scatter_custom_fusion
  47.0 2.6 scatter_custom_fusion.1
  50.3 8.3 %all-to-all-start = ((s32[16,2,32]{2,1,0:T(2,128)}), s32[16,2,32]{2,1,0:T(2,128)S(1)}, u32[]{:S(2)}, u32[]{:S(2)}) async-start(s32[16,2,32]{2,1,0:T(2,128)} %reshape.1434), calls=%async_computation | async-start | bytes 32768 | tf_op jit(solution)/shard_map/all_to_all | solution.py:87
  59.1 6.9 %all-to-all-done = s32[16,2,32]{2,1,0:T(2,128)S(1)} async-done(((s32[16,2,32]{2,1,0:T(2,128)}), s32[16,2,32]{2,1,0:T(2,128)S(1)}, u32[]{:S(2)}, u32[]{:S(2)}) %all-to-all-start) | async-done | bytes 4128 | tf_op jit(solution)/shard_map/all_to_all | solution.py:87
  66.1 3.7 %all_to_all.30 = s32[2,1,512]{2,1,0:T(1,128)S(1)} all-to-all(s32[2,1,512]{2,1,0:T(1,128)S(1)} %reshape.1574), channel_id=1, replica_groups=mesh['track'=16,'cam'=2] {'cam'}, dimensions={0} | all-to-all | bytes 8192 | tf_op jit(solution)/shard_map/all_to_all | solution.py:86
  71.2 8.3 %gather_fusion.2 = bf16[1024,32,9]{1,2,0:T(8,128)(2,1)} fusion(bf16[32,9,128]{0,1,2:T(8,128)(2,1)S(1)} %copy.264, s32[1024]{0:T(1024)S(1)} %broadcast_clamp_fusion), kind=kCustom, calls=%fused_computation.2 | custom fusion | bytes 1183744 | tf_op jit(solution)/shard_map/jit(_take)/gather | solution.py:97
  79.5 2.8 fusion
  82.3 2.5 reshape.1437
  84.7 1.4 copy.271
  86.2 3.6 all-to-all-start.2
  98.8 7.5 %all-to-all-done.2 = bf16[16,2,9,1024]{3,1,2,0:T(2,128)(2,1)S(1)} async-done(((bf16[16,2,9,1024]{3,1,2,0:T(2,128)(2,1)}), bf16[16,2,9,1024]{3,1,2,0:T(2,128)(2,1)S(1)}, u32[]{:S(2)}, u32[]{:S(2)}) %all-to-all-start.2) | async-done | bytes 589856 | tf_op jit(solution)/shard_map/all_to_all | solution.py:104
  106.5 4.2 %all_to_all.31 = bf16[16,2,9,1024]{3,0,2,1:T(8,128)(2,1)S(1)} all-to-all(bf16[16,2,9,1024]{3,0,2,1:T(8,128)(2,1)S(1)} %copy.272), channel_id=1, replica_groups=mesh['track'=16,'cam'=2] {'cam'}, dimensions={1} | all-to-all | bytes 1179648 | tf_op jit(solution)/shard_map/all_to_all | solution.py:103
  110.7 1.8 reshape.1438
  112.5 4.9 %copy.328 = bf16[9,32,16,2,32]{1,0,4,3,2:T(8,128)(2,1)} copy(bf16[9,32,16,2,32]{1,4,2,0,3:T(8,128)(2,1)S(1)} %bitcast.143) | data formatting | bytes 1179648 | tf_op jit(solution)/shard_map/reshape | solution.py:113
  117.6 3.4 gather_fusion.3
  121.1 1.2 copy.275
  124.4 2.0 copy.310
  126.4 2.5 broadcast_in_dim.74
  128.9 47.3 %scatter_fusion = bf16[9,32,1024]{1,0,2:T(8,128)(2,1)} fusion(bf16[9,32,1024]{1,0,2:T(8,128)(2,1)} %broadcast_in_dim.74, s32[512]{0:T(512)S(1)} %copy-done.25, bf16[512,9,32]{2,1,0:T(8,128)(2,1)S(1)} %copy.310), kind=kCustom, calls=%fused_computation.6 | custom fusion | bytes 886784 | tf_op jit(solution)/shard_map/scatter | solution.py:120
  176.2 2.8 copy.379
  179.0 2.5 reshape.1441
  181.5 1.4 copy.312
  183.0 4.4 %all-to-all-start.4 = ((bf16[16,2,9,1024]{3,1,2,0:T(2,128)(2,1)}), bf16[16,2,9,1024]{3,1,2,0:T(2,128)(2,1)S(1)}, u32[]{:S(2)}, u32[]{:S(2)}) async-start(bf16[16,2,9,1024]{3,1,2,0:T(2,128)(2,1)} %copy.312), calls=%async_computation.4 | async-start | bytes 1179648 | tf_op jit(solution)/shard_map/all_to_all | solution.py:128
  187.4 1.4 copy.265
  188.9 15.1 %all-to-all-done.4 = bf16[16,2,9,1024]{3,1,2,0:T(2,128)(2,1)S(1)} async-done(((bf16[16,2,9,1024]{3,1,2,0:T(2,128)(2,1)}), bf16[16,2,9,1024]{3,1,2,0:T(2,128)(2,1)S(1)}, u32[]{:S(2)}, u32[]{:S(2)}) %all-to-all-start.4) | async-done | bytes 589856 | tf_op jit(solution)/shard_map/all_to_all | solution.py:128
  204.2 4.2 %all_to_all.32 = bf16[16,2,9,1024]{3,0,2,1:T(8,128)(2,1)S(1)} all-to-all(bf16[16,2,9,1024]{3,0,2,1:T(8,128)(2,1)S(1)} %copy.313), channel_id=1, replica_groups=mesh['track'=16,'cam'=2] {'cam'}, dimensions={1} | all-to-all | bytes 1179648 | tf_op jit(solution)/shard_map/all_to_all | solution.py:127
  208.4 2.8 reshape.1444
  211.2 7.7 %copy.314 = f32[32,9,16,2,32]{4,3,2,0,1:T(2,128)} copy(f32[32,9,16,2,32]{0,4,2,1,3:T(8,128)} %bitcast.141) | data formatting | bytes 2359296 | tf_op jit(solution)/shard_map/convert_element_type | solution.py:138
  218.9 6.9 %reshape.1502 = f32[32,9,1024]{2,0,1:T(8,128)S(1)} reshape(f32[32,9,16,2,32]{4,3,2,0,1:T(2,128)} %copy.314) | data formatting | bytes 2359296 | tf_op jit(solution)/shard_map/convert_element_type | solution.py:138
  225.8 6.1 %copy.315 = f32[1024,32,9]{1,2,0:T(8,128)} copy(f32[1024,32,9]{0,1,2:T(8,128)S(1)} %bitcast.174) | data formatting | bytes 2359296 | tf_op jit(solution)/shard_map/convert_element_type | solution.py:138
  232.0 81.2 %scatter_fusion.1 = f32[32,9,129]{0,1,2:T(8,128)S(1)} fusion(f32[32,9,129]{0,1,2:T(8,128)S(1)} %broadcast_in_dim.67, s32[1024]{0:T(1024)S(1)} %bitcast.234, f32[1024,32,9]{1,2,0:T(8,128)} %copy.315), kind=kCustom, calls=%fused_computation.7 | custom fusion | flops 294912 | bytes 3543040 | tf_op jit(solution)/shard_map/scatter-add | solution.py:144
  313.2 1.9 fusion.1
  316.1 39.3 %psum.7 = f32[32,32]{0,1:T(8,128)S(1)} all-reduce(f32[32,32]{0,1:T(8,128)S(1)} %convolution_bitcast_fusion.2), channel_id=1, replica_groups=mesh['track'=16,'cam'=2] {'track','cam'}, use_global_device_ids=true, to_apply=%region_7.8 | all-reduce | flops 1024 | bytes 8192 | tf_op jit(solution)/shard_map/psum | solution.py:151
  355.5 2.9 cholesky.16
  359.8 2.4 custom-call.7
  (209 shorter events, 19.2 us)
Async XLA Ops:
  8.6 50.0 %copy-start.2 = (bf16[32,9,128]{2,0,1:T(8,128)(2,1)S(1)}, bf16[32,9,128]{2,0,1:T(8,128)(2,1)}, u32[]{:S(2)}) copy-start(bf16[32,9,128]{2,0,1:T(8,128)(2,1)} %param.9) | copy-start | bytes 221188
  47.0 48.8 %copy-start.24 = (s32[512]{0:T(512)}, s32[512]{0:T(512)S(1)}, u32[]{:S(2)}) copy-start(s32[512]{0:T(512)S(1)} %compare_select_fusion.3) | copy-start | bytes 6148
  50.3 15.7 %all-to-all-start = ((s32[16,2,32]{2,1,0:T(2,128)}), s32[16,2,32]{2,1,0:T(2,128)S(1)}, u32[]{:S(2)}, u32[]{:S(2)}) async-start(s32[16,2,32]{2,1,0:T(2,128)} %reshape.1434), calls=%async_computation | async-start | bytes 32768 | tf_op jit(solution)/shard_map/all_to_all | solution.py:87
  82.2 7.5 %copy-start.39 = (f32[3,3,128]{2,1,0:T(4,128)S(1)}, f32[3,3,128]{2,1,0:T(4,128)}, u32[]{:S(2)}) copy-start(f32[3,3,128]{2,1,0:T(4,128)} %param.12) | copy-start | bytes 13828
  82.2 14.7 %copy-start.41 = (s32[512]{0:T(512)S(1)}, s32[512]{0:T(512)}, u32[]{:S(2)}) copy-start(s32[512]{0:T(512)} %param.15) | copy-start | bytes 6148
  82.2 15.3 %copy-start.1 = (bf16[9,3,512]{2,1,0:T(4,128)(2,1)S(1)}, bf16[9,3,512]{2,1,0:T(4,128)(2,1)}, u32[]{:S(2)}) copy-start(bf16[9,3,512]{2,1,0:T(4,128)(2,1)} %param.11) | copy-start | bytes 82948
  86.2 20.2 %all-to-all-start.2 = ((bf16[16,2,9,1024]{3,1,2,0:T(2,128)(2,1)}), bf16[16,2,9,1024]{3,1,2,0:T(2,128)(2,1)S(1)}, u32[]{:S(2)}, u32[]{:S(2)}) async-start(bf16[16,2,9,1024]{3,1,2,0:T(2,128)(2,1)} %copy.271), calls=%async_computation.2 | async-start | bytes 1179648 | tf_op jit(solution)/shard_map/all_to_all | solution.py:104
  112.5 5.1 %copy-start.26 = (s32[1024]{0:T(1024)S(1)}, s32[1024]{0:T(1024)}, u32[]{:S(2)}) copy-start(s32[1024]{0:T(1024)} %pad_clamp_fusion.1) | copy-start | bytes 12292
  117.4 4.9 %copy-start.40 = (pred[512]{0:T(512)(128)(4,1)S(1)}, pred[512]{0:T(512)(128)(4,1)}, u32[]{:S(2)}) copy-start(pred[512]{0:T(512)(128)(4,1)} %compare_and_fusion.1) | copy-start | bytes 1540
  117.4 5.0 %copy-start.5 = (f32[1,1,512]{2,1,0:T(1,128)S(1)}, f32[1,1,512]{2,1,0:T(1,128)}, u32[]{:S(2)}) copy-start(f32[1,1,512]{2,1,0:T(1,128)} %get-tuple-element.140) | copy-start | bytes 6148
  117.4 5.0 %copy-start.8 = (f32[1,1,512]{2,1,0:T(1,128)S(1)}, f32[1,1,512]{2,1,0:T(1,128)}, u32[]{:S(2)}) copy-start(f32[1,1,512]{2,1,0:T(1,128)} %get-tuple-element.139) | copy-start | bytes 6148
  117.4 5.0 %copy-start.10 = (f32[1,1,512]{2,1,0:T(1,128)S(1)}, f32[1,1,512]{2,1,0:T(1,128)}, u32[]{:S(2)}) copy-start(f32[1,1,512]{2,1,0:T(1,128)} %get-tuple-element.138) | copy-start | bytes 6148
  117.4 5.0 %copy-start.13 = (f32[1,1,512]{2,1,0:T(1,128)S(1)}, f32[1,1,512]{2,1,0:T(1,128)}, u32[]{:S(2)}) copy-start(f32[1,1,512]{2,1,0:T(1,128)} %get-tuple-element.137) | copy-start | bytes 6148
  117.4 5.0 %copy-start.15 = (f32[1,1,512]{2,1,0:T(1,128)S(1)}, f32[1,1,512]{2,1,0:T(1,128)}, u32[]{:S(2)}) copy-start(f32[1,1,512]{2,1,0:T(1,128)} %get-tuple-element.136) | copy-start | bytes 6148
  117.4 5.0 %copy-start.17 = (f32[1,1,512]{2,1,0:T(1,128)S(1)}, f32[1,1,512]{2,1,0:T(1,128)}, u32[]{:S(2)}) copy-start(f32[1,1,512]{2,1,0:T(1,128)} %get-tuple-element.135) | copy-start | bytes 6148
  117.4 5.0 %copy-start.19 = (f32[1,1,512]{2,1,0:T(1,128)S(1)}, f32[1,1,512]{2,1,0:T(1,128)}, u32[]{:S(2)}) copy-start(f32[1,1,512]{2,1,0:T(1,128)} %get-tuple-element.134) | copy-start | bytes 6148
  117.5 5.0 %copy-start.21 = (f32[1,1,512]{2,1,0:T(1,128)S(1)}, f32[1,1,512]{2,1,0:T(1,128)}, u32[]{:S(2)}) copy-start(f32[1,1,512]{2,1,0:T(1,128)} %get-tuple-element.133) | copy-start | bytes 6148
  117.5 5.0 %copy-start.4 = (f32[1,1,512]{2,1,0:T(1,128)S(1)}, f32[1,1,512]{2,1,0:T(1,128)}, u32[]{:S(2)}) copy-start(f32[1,1,512]{2,1,0:T(1,128)} %get-tuple-element.154) | copy-start | bytes 6148
  117.5 5.0 %copy-start.6 = (f32[1,1,512]{2,1,0:T(1,128)S(1)}, f32[1,1,512]{2,1,0:T(1,128)}, u32[]{:S(2)}) copy-start(f32[1,1,512]{2,1,0:T(1,128)} %get-tuple-element.149) | copy-start | bytes 6148
  117.5 5.0 %copy-start.7 = (f32[1,1,512]{2,1,0:T(1,128)S(1)}, f32[1,1,512]{2,1,0:T(1,128)}, u32[]{:S(2)}) copy-start(f32[1,1,512]{2,1,0:T(1,128)} %get-tuple-element.153) | copy-start | bytes 6148
  117.5 5.0 %copy-start.9 = (f32[1,1,512]{2,1,0:T(1,128)S(1)}, f32[1,1,512]{2,1,0:T(1,128)}, u32[]{:S(2)}) copy-start(f32[1,1,512]{2,1,0:T(1,128)} %get-tuple-element.148) | copy-start | bytes 6148
  117.5 5.0 %copy-start.11 = (f32[1,1,512]{2,1,0:T(1,128)S(1)}, f32[1,1,512]{2,1,0:T(1,128)}, u32[]{:S(2)}) copy-start(f32[1,1,512]{2,1,0:T(1,128)} %get-tuple-element.147) | copy-start | bytes 6148
  117.5 5.0 %copy-start.12 = (f32[1,1,512]{2,1,0:T(1,128)S(1)}, f32[1,1,512]{2,1,0:T(1,128)}, u32[]{:S(2)}) copy-start(f32[1,1,512]{2,1,0:T(1,128)} %get-tuple-element.152) | copy-start | bytes 6148
  117.5 5.0 %copy-start.14 = (f32[1,1,512]{2,1,0:T(1,128)S(1)}, f32[1,1,512]{2,1,0:T(1,128)}, u32[]{:S(2)}) copy-start(f32[1,1,512]{2,1,0:T(1,128)} %get-tuple-element.146) | copy-start | bytes 6148
  117.5 5.0 %copy-start.16 = (f32[1,1,512]{2,1,0:T(1,128)S(1)}, f32[1,1,512]{2,1,0:T(1,128)}, u32[]{:S(2)}) copy-start(f32[1,1,512]{2,1,0:T(1,128)} %get-tuple-element.145) | copy-start | bytes 6148
  117.6 5.0 %copy-start.18 = (f32[1,1,512]{2,1,0:T(1,128)S(1)}, f32[1,1,512]{2,1,0:T(1,128)}, u32[]{:S(2)}) copy-start(f32[1,1,512]{2,1,0:T(1,128)} %get-tuple-element.144) | copy-start | bytes 6148
  117.6 5.0 %copy-start.20 = (f32[1,1,512]{2,1,0:T(1,128)S(1)}, f32[1,1,512]{2,1,0:T(1,128)}, u32[]{:S(2)}) copy-start(f32[1,1,512]{2,1,0:T(1,128)} %get-tuple-element.143) | copy-start | bytes 6148
  117.6 5.0 %copy-start.22 = (f32[1,1,512]{2,1,0:T(1,128)S(1)}, f32[1,1,512]{2,1,0:T(1,128)}, u32[]{:S(2)}) copy-start(f32[1,1,512]{2,1,0:T(1,128)} %get-tuple-element.142) | copy-start | bytes 6148
  117.6 5.0 %copy-start.23 = (f32[1,1,512]{2,1,0:T(1,128)S(1)}, f32[1,1,512]{2,1,0:T(1,128)}, u32[]{:S(2)}) copy-start(f32[1,1,512]{2,1,0:T(1,128)} %get-tuple-element.151) | copy-start | bytes 6148
  121.0 1.8 copy-start.27
  121.0 1.8 copy-start.29
  121.0 2.2 copy-start.30
  121.0 2.2 copy-start.31
  121.0 2.2 copy-start.32
  121.0 2.2 copy-start.33
  121.0 2.2 copy-start.34
  121.1 2.2 copy-start.35
  121.1 2.2 copy-start.36
  121.1 2.2 copy-start.37
  121.1 2.2 copy-start.38
  123.3 1.1 copy-start.28
  126.4 2.5 copy-start.25
  181.5 5.9 %copy-start.3 = (f32[9,9,128]{2,1,0:T(8,128)S(1)}, f32[9,9,128]{2,1,0:T(8,128)}, u32[]{:S(2)}) copy-start(f32[9,9,128]{2,1,0:T(8,128)} %param.10) | copy-start | bytes 124420
  183.0 21.1 %all-to-all-start.4 = ((bf16[16,2,9,1024]{3,1,2,0:T(2,128)(2,1)}), bf16[16,2,9,1024]{3,1,2,0:T(2,128)(2,1)S(1)}, u32[]{:S(2)}, u32[]{:S(2)}) async-start(bf16[16,2,9,1024]{3,1,2,0:T(2,128)(2,1)} %copy.312), calls=%async_computation.4 | async-start | bytes 1179648 | tf_op jit(solution)/shard_map/all_to_all | solution.py:128
  315.4 48.6 %copy-start = (f32[32,9,128]{2,0,1:T(8,128)}, f32[32,9,128]{2,0,1:T(8,128)S(1)}, u32[]{:S(2)}) copy-start(f32[32,9,128]{2,0,1:T(8,128)S(1)} %copy.323) | copy-start | bytes 442372
where the time goes:
time: 367 us; the launch traced here: 364 us
  local copies, waits for them, and re-layouts  162 us (44%)
  other arithmetic  98.7 us (27%)
  blocking collectives  51.4 us (14%)
  waiting for transfers between devices  29.5 us (8%)
  starting transfers between devices  16.4 us (4%)
  matrix products  3.83 us (1%)
    scatter-add x1, other arithmetic, on_device(): incoming = jnp.zeros((columns, params, table_width + 1), jnp.float32).at[...  81.2 us
    scatter x1, local copies, waits for them, and re-layouts, on_device(): buffer = jnp.zeros((params, columns, buffer_slots), jnp.bfloat16).at[:, :...  47.3 us
    psum x1, blocking collectives, on_device(): lax.psum(gram_local, ('track', 'cam')) / row_total  39.3 us
    gather x10, local copies, waits for them, and re-layouts, on_device(): first_index = jnp.searchsorted(ranked, ranked, side='left')  34.9 us
    convert_element_type x4, local copies, waits for them, and re-layouts, on_device(): terms = arrived.reshape(track_count, cam_count, params, capacity, columns...  23.6 us
    all_to_all x1, waiting for transfers between devices, on_device(): lax.all_to_all(packed, 'track', split_axis=0, concat_axis=0, tiled=True)  15.1 us
    all_to_all x1, starting transfers between devices, on_device(): lax.all_to_all(request, 'track', split_axis=0, concat_axis=0, tiled=True)  8.34 us
    gather x1, local copies, waits for them, and re-layouts, on_device(): gathered_rows = jnp.take(omega, local_ids, axis=2)  8.28 us
  transfers between devices with their start and end apart: 3, of which 3 were waited for; matrix products, arithmetic and copies ran while one was open for 3% of the time, Pallas kernels for 0%

commit v1 on v0

--- a/solution.py
+++ b/solution.py
@@ -148,7 +148,7 @@
     flat_rows = sketch.reshape(columns, params * cam_width)
     gram_local = jnp.dot(flat_rows, flat_rows.T, precision=HIGH, preferred_element_type=jnp.float32)
     row_total = params * cam_width * devices
-    lower_factor = jnp.linalg.cholesky(lax.psum(gram_local, ("track", "cam")) / row_total)
+    lower_factor = jnp.linalg.cholesky(lax.psum(lax.psum(gram_local, "cam"), "track") / row_total)
     basis_rows = jax.scipy.linalg.solve_triangular(lower_factor, flat_rows, lower=True).reshape(
         sketch.shape
     )

time: 367 us -> 406 us (1.11)
  blocking collectives: 51.4 us -> 89.9 us
    psum x1 -> x2, blocking collectives: 39.3 us -> 77.8 us  [the longest x1 74.4 us: on_device(): lax.psum(lax.psum(gram_local, 'cam'), 'track') / row_total]
where the time goes in v1:
time: 406 us; the launch traced here: 402 us
  local copies, waits for them, and re-layouts  162 us (40%)
  other arithmetic  98.6 us (24%)
  blocking collectives  89.9 us (22%)
  waiting for transfers between devices  29.5 us (7%)
  starting transfers between devices  16.2 us (4%)
    scatter-add x1, other arithmetic, on_device(): incoming = jnp.zeros((columns, params, table_width + 1), jnp.float32).at[...  81.2 us
    psum x1, blocking collectives, on_device(): lax.psum(lax.psum(gram_local, 'cam'), 'track') / row_total  74.4 us
    scatter x1, local copies, waits for them, and re-layouts, on_device(): buffer = jnp.zeros((params, columns, buffer_slots), jnp.bfloat16).at[:, :...  47.5 us
    gather x10, local copies, waits for them, and re-layouts, on_device(): first_index = jnp.searchsorted(ranked, ranked, side='left')  34.9 us
    convert_element_type x4, local copies, waits for them, and re-layouts, on_device(): terms = arrived.reshape(track_count, cam_count, params, capacity, columns...  23.6 us
    all_to_all x1, waiting for transfers between devices, on_device(): lax.all_to_all(packed, 'track', split_axis=0, concat_axis=0, tiled=True)  15 us
    gather x1, local copies, waits for them, and re-layouts, on_device(): gathered_rows = jnp.take(omega, local_ids, axis=2)  8.35 us
    all_to_all x1, starting transfers between devices, on_device(): lax.all_to_all(request, 'track', split_axis=0, concat_axis=0, tiled=True)  8.34 us
  transfers between devices with their start and end apart: 3, of which 3 were waited for; matrix products, arithmetic and copies ran while one was open for 3% of the time, Pallas kernels for 0%

profile of v1, /device:TPU:0, one launch (start us, length us, event | category | flops | bytes accessed | tf_op | source)
XLA Modules:
  0.0 402.4 jit_solution(1331365375634229943)
XLA Ops:
  1.3 3.8 sort.17
  5.1 3.5 gather_fusion.1
  8.6 35.9 %while.25 = (s32[]{:T(128)}, u32[512]{0:T(512)S(1)}, u32[512]{0:T(512)S(1)}, s32[512]{0:T(512)S(1)}, s32[]{:T(128)}, /*index=5*/s32[]{:T(128)}, s32[]{}) while((s32[]{:T(128)}, u32[512]{0:T(512)S(1)}, u32[512]{0:T(512)S(1)}, s32[512]{0:T(512)S(1)}, s32[]{:T(128)}, /*index=5*/s32[]{:T(128)}, s32[]{}) %tuple.87), condition=%wide.region_2.3_spmd.clone, body=%wide.region_1.2_spmd.clone.sunk | while | flops 10244 | bytes 40037 | solution.py:77
  8.7 3.5 gather_fusion
  12.3 3.5 gather_fusion
  15.9 3.5 gather_fusion
  19.4 3.5 gather_fusion
  23.0 3.5 gather_fusion
  26.6 3.5 gather_fusion
  30.2 3.5 gather_fusion
  33.8 3.5 gather_fusion
  37.4 3.5 gather_fusion
  41.0 3.5 gather_fusion
  44.5 2.4 scatter_custom_fusion
  47.0 2.6 scatter_custom_fusion.1
  50.3 8.3 %all-to-all-start = ((s32[16,2,32]{2,1,0:T(2,128)}), s32[16,2,32]{2,1,0:T(2,128)S(1)}, u32[]{:S(2)}, u32[]{:S(2)}) async-start(s32[16,2,32]{2,1,0:T(2,128)} %reshape.1434), calls=%async_computation | async-start | bytes 32768 | tf_op jit(solution)/shard_map/all_to_all | solution.py:87
  59.1 6.9 %all-to-all-done = s32[16,2,32]{2,1,0:T(2,128)S(1)} async-done(((s32[16,2,32]{2,1,0:T(2,128)}), s32[16,2,32]{2,1,0:T(2,128)S(1)}, u32[]{:S(2)}, u32[]{:S(2)}) %all-to-all-start) | async-done | bytes 4128 | tf_op jit(solution)/shard_map/all_to_all | solution.py:87
  66.1 3.7 all_to_all.30
  71.2 8.3 %gather_fusion.2 = bf16[1024,32,9]{1,2,0:T(8,128)(2,1)} fusion(bf16[32,9,128]{0,1,2:T(8,128)(2,1)S(1)} %copy.264, s32[1024]{0:T(1024)S(1)} %broadcast_clamp_fusion), kind=kCustom, calls=%fused_computation.2 | custom fusion | bytes 1183744 | tf_op jit(solution)/shard_map/jit(_take)/gather | solution.py:97
  79.5 2.8 fusion
  82.3 2.5 reshape.1437
  84.8 1.4 copy.271
  86.2 3.6 all-to-all-start.2
  98.8 7.6 %all-to-all-done.2 = bf16[16,2,9,1024]{3,1,2,0:T(2,128)(2,1)S(1)} async-done(((bf16[16,2,9,1024]{3,1,2,0:T(2,128)(2,1)}), bf16[16,2,9,1024]{3,1,2,0:T(2,128)(2,1)S(1)}, u32[]{:S(2)}, u32[]{:S(2)}) %all-to-all-start.2) | async-done | bytes 589856 | tf_op jit(solution)/shard_map/all_to_all | solution.py:104
  106.5 4.2 %all_to_all.31 = bf16[16,2,9,1024]{3,0,2,1:T(8,128)(2,1)S(1)} all-to-all(bf16[16,2,9,1024]{3,0,2,1:T(8,128)(2,1)S(1)} %copy.272), channel_id=1, replica_groups=mesh['track'=16,'cam'=2] {'cam'}, dimensions={1} | all-to-all | bytes 1179648 | tf_op jit(solution)/shard_map/all_to_all | solution.py:103
  110.8 1.8 reshape.1438
  112.6 4.9 %copy.328 = bf16[9,32,16,2,32]{1,0,4,3,2:T(8,128)(2,1)} copy(bf16[9,32,16,2,32]{1,4,2,0,3:T(8,128)(2,1)S(1)} %bitcast.143) | data formatting | bytes 1179648 | tf_op jit(solution)/shard_map/reshape | solution.py:113
  117.7 3.4 gather_fusion.3
  124.5 2.0 copy.310
  126.5 2.5 broadcast_in_dim.74
  129.0 47.5 %scatter_fusion = bf16[9,32,1024]{1,0,2:T(8,128)(2,1)} fusion(bf16[9,32,1024]{1,0,2:T(8,128)(2,1)} %broadcast_in_dim.74, s32[512]{0:T(512)S(1)} %copy-done.25, bf16[512,9,32]{2,1,0:T(8,128)(2,1)S(1)} %copy.310), kind=kCustom, calls=%fused_computation.6 | custom fusion | bytes 886784 | tf_op jit(solution)/shard_map/scatter | solution.py:120
  176.5 2.8 copy.379
  179.3 2.5 reshape.1441
  181.8 1.4 copy.312
  183.2 4.2 %all-to-all-start.4 = ((bf16[16,2,9,1024]{3,1,2,0:T(2,128)(2,1)}), bf16[16,2,9,1024]{3,1,2,0:T(2,128)(2,1)S(1)}, u32[]{:S(2)}, u32[]{:S(2)}) async-start(bf16[16,2,9,1024]{3,1,2,0:T(2,128)(2,1)} %copy.312), calls=%async_computation.4 | async-start | bytes 1179648 | tf_op jit(solution)/shard_map/all_to_all | solution.py:128
  187.5 1.4 copy.265
  189.0 15.0 %all-to-all-done.4 = bf16[16,2,9,1024]{3,1,2,0:T(2,128)(2,1)S(1)} async-done(((bf16[16,2,9,1024]{3,1,2,0:T(2,128)(2,1)}), bf16[16,2,9,1024]{3,1,2,0:T(2,128)(2,1)S(1)}, u32[]{:S(2)}, u32[]{:S(2)}) %all-to-all-start.4) | async-done | bytes 589856 | tf_op jit(solution)/shard_map/all_to_all | solution.py:128
  204.2 4.2 %all_to_all.32 = bf16[16,2,9,1024]{3,0,2,1:T(8,128)(2,1)S(1)} all-to-all(bf16[16,2,9,1024]{3,0,2,1:T(8,128)(2,1)S(1)} %copy.313), channel_id=1, replica_groups=mesh['track'=16,'cam'=2] {'cam'}, dimensions={1} | all-to-all | bytes 1179648 | tf_op jit(solution)/shard_map/all_to_all | solution.py:127
  208.4 2.8 reshape.1444
  211.2 7.7 %copy.314 = f32[32,9,16,2,32]{4,3,2,0,1:T(2,128)} copy(f32[32,9,16,2,32]{0,4,2,1,3:T(8,128)} %bitcast.141) | data formatting | bytes 2359296 | tf_op jit(solution)/shard_map/convert_element_type | solution.py:138
  218.9 6.9 %reshape.1502 = f32[32,9,1024]{2,0,1:T(8,128)S(1)} reshape(f32[32,9,16,2,32]{4,3,2,0,1:T(2,128)} %copy.314) | data formatting | bytes 2359296 | tf_op jit(solution)/shard_map/convert_element_type | solution.py:138
  225.8 6.2 %copy.315 = f32[1024,32,9]{1,2,0:T(8,128)} copy(f32[1024,32,9]{0,1,2:T(8,128)S(1)} %bitcast.174) | data formatting | bytes 2359296 | tf_op jit(solution)/shard_map/convert_element_type | solution.py:138
  232.1 81.2 %scatter_fusion.1 = f32[32,9,129]{0,1,2:T(8,128)S(1)} fusion(f32[32,9,129]{0,1,2:T(8,128)S(1)} %broadcast_in_dim.67, s32[1024]{0:T(1024)S(1)} %bitcast.234, f32[1024,32,9]{1,2,0:T(8,128)} %copy.315), kind=kCustom, calls=%fused_computation.7 | custom fusion | flops 294912 | bytes 3543040 | tf_op jit(solution)/shard_map/scatter-add | solution.py:144
  313.2 1.9 fusion.1
  316.2 3.4 psum.14
  319.6 74.4 %psum.15 = f32[32,32]{0,1:T(8,128)S(1)} all-reduce(f32[32,32]{0,1:T(8,128)S(1)} %psum.14), channel_id=1, replica_groups=mesh['track'=16,'cam'=2] {'track'}, use_global_device_ids=true, to_apply=%region_8.9 | all-reduce | flops 1024 | bytes 8192 | tf_op jit(solution)/shard_map/psum | solution.py:151
  394.0 2.9 cholesky.16
  398.3 2.4 custom-call.7
  (210 shorter events, 20.3 us)
Async XLA Ops:
  8.6 50.0 %copy-start.2 = (bf16[32,9,128]{2,0,1:T(8,128)(2,1)S(1)}, bf16[32,9,128]{2,0,1:T(8,128)(2,1)}, u32[]{:S(2)}) copy-start(bf16[32,9,128]{2,0,1:T(8,128)(2,1)} %param.9) | copy-start | bytes 221188
  47.0 48.8 %copy-start.24 = (s32[512]{0:T(512)}, s32[512]{0:T(512)S(1)}, u32[]{:S(2)}) copy-start(s32[512]{0:T(512)S(1)} %compare_select_fusion.3) | copy-start | bytes 6148
  50.3 15.7 %all-to-all-start = ((s32[16,2,32]{2,1,0:T(2,128)}), s32[16,2,32]{2,1,0:T(2,128)S(1)}, u32[]{:S(2)}, u32[]{:S(2)}) async-start(s32[16,2,32]{2,1,0:T(2,128)} %reshape.1434), calls=%async_computation | async-start | bytes 32768 | tf_op jit(solution)/shard_map/all_to_all | solution.py:87
  82.3 7.5 %copy-start.39 = (f32[3,3,128]{2,1,0:T(4,128)S(1)}, f32[3,3,128]{2,1,0:T(4,128)}, u32[]{:S(2)}) copy-start(f32[3,3,128]{2,1,0:T(4,128)} %param.12) | copy-start | bytes 13828
  82.3 14.6 %copy-start.41 = (s32[512]{0:T(512)S(1)}, s32[512]{0:T(512)}, u32[]{:S(2)}) copy-start(s32[512]{0:T(512)} %param.15) | copy-start | bytes 6148
  82.3 15.2 %copy-start.1 = (bf16[9,3,512]{2,1,0:T(4,128)(2,1)S(1)}, bf16[9,3,512]{2,1,0:T(4,128)(2,1)}, u32[]{:S(2)}) copy-start(bf16[9,3,512]{2,1,0:T(4,128)(2,1)} %param.11) | copy-start | bytes 82948
  86.2 20.2 %all-to-all-start.2 = ((bf16[16,2,9,1024]{3,1,2,0:T(2,128)(2,1)}), bf16[16,2,9,1024]{3,1,2,0:T(2,128)(2,1)S(1)}, u32[]{:S(2)}, u32[]{:S(2)}) async-start(bf16[16,2,9,1024]{3,1,2,0:T(2,128)(2,1)} %copy.271), calls=%async_computation.2 | async-start | bytes 1179648 | tf_op jit(solution)/shard_map/all_to_all | solution.py:104
  112.6 5.1 %copy-start.26 = (s32[1024]{0:T(1024)S(1)}, s32[1024]{0:T(1024)}, u32[]{:S(2)}) copy-start(s32[1024]{0:T(1024)} %pad_clamp_fusion.1) | copy-start | bytes 12292
  117.5 4.9 %copy-start.40 = (pred[512]{0:T(512)(128)(4,1)S(1)}, pred[512]{0:T(512)(128)(4,1)}, u32[]{:S(2)}) copy-start(pred[512]{0:T(512)(128)(4,1)} %compare_and_fusion.1) | copy-start | bytes 1540
  117.5 5.0 %copy-start.5 = (f32[1,1,512]{2,1,0:T(1,128)S(1)}, f32[1,1,512]{2,1,0:T(1,128)}, u32[]{:S(2)}) copy-start(f32[1,1,512]{2,1,0:T(1,128)} %get-tuple-element.140) | copy-start | bytes 6148
  117.5 5.0 %copy-start.8 = (f32[1,1,512]{2,1,0:T(1,128)S(1)}, f32[1,1,512]{2,1,0:T(1,128)}, u32[]{:S(2)}) copy-start(f32[1,1,512]{2,1,0:T(1,128)} %get-tuple-element.139) | copy-start | bytes 6148
  117.5 5.0 %copy-start.10 = (f32[1,1,512]{2,1,0:T(1,128)S(1)}, f32[1,1,512]{2,1,0:T(1,128)}, u32[]{:S(2)}) copy-start(f32[1,1,512]{2,1,0:T(1,128)} %get-tuple-element.138) | copy-start | bytes 6148
  117.5 5.0 %copy-start.13 = (f32[1,1,512]{2,1,0:T(1,128)S(1)}, f32[1,1,512]{2,1,0:T(1,128)}, u32[]{:S(2)}) copy-start(f32[1,1,512]{2,1,0:T(1,128)} %get-tuple-element.137) | copy-start | bytes 6148
  117.5 5.0 %copy-start.15 = (f32[1,1,512]{2,1,0:T(1,128)S(1)}, f32[1,1,512]{2,1,0:T(1,128)}, u32[]{:S(2)}) copy-start(f32[1,1,512]{2,1,0:T(1,128)} %get-tuple-element.136) | copy-start | bytes 6148
  117.5 5.0 %copy-start.17 = (f32[1,1,512]{2,1,0:T(1,128)S(1)}, f32[1,1,512]{2,1,0:T(1,128)}, u32[]{:S(2)}) copy-start(f32[1,1,512]{2,1,0:T(1,128)} %get-tuple-element.135) | copy-start | bytes 6148
  117.5 5.0 %copy-start.19 = (f32[1,1,512]{2,1,0:T(1,128)S(1)}, f32[1,1,512]{2,1,0:T(1,128)}, u32[]{:S(2)}) copy-start(f32[1,1,512]{2,1,0:T(1,128)} %get-tuple-element.134) | copy-start | bytes 6148
  117.5 5.0 %copy-start.21 = (f32[1,1,512]{2,1,0:T(1,128)S(1)}, f32[1,1,512]{2,1,0:T(1,128)}, u32[]{:S(2)}) copy-start(f32[1,1,512]{2,1,0:T(1,128)} %get-tuple-element.133) | copy-start | bytes 6148
  117.5 5.0 %copy-start.4 = (f32[1,1,512]{2,1,0:T(1,128)S(1)}, f32[1,1,512]{2,1,0:T(1,128)}, u32[]{:S(2)}) copy-start(f32[1,1,512]{2,1,0:T(1,128)} %get-tuple-element.154) | copy-start | bytes 6148
  117.5 5.0 %copy-start.6 = (f32[1,1,512]{2,1,0:T(1,128)S(1)}, f32[1,1,512]{2,1,0:T(1,128)}, u32[]{:S(2)}) copy-start(f32[1,1,512]{2,1,0:T(1,128)} %get-tuple-element.149) | copy-start | bytes 6148
  117.6 5.0 %copy-start.7 = (f32[1,1,512]{2,1,0:T(1,128)S(1)}, f32[1,1,512]{2,1,0:T(1,128)}, u32[]{:S(2)}) copy-start(f32[1,1,512]{2,1,0:T(1,128)} %get-tuple-element.153) | copy-start | bytes 6148
  117.6 5.0 %copy-start.9 = (f32[1,1,512]{2,1,0:T(1,128)S(1)}, f32[1,1,512]{2,1,0:T(1,128)}, u32[]{:S(2)}) copy-start(f32[1,1,512]{2,1,0:T(1,128)} %get-tuple-element.148) | copy-start | bytes 6148
  117.6 5.0 %copy-start.11 = (f32[1,1,512]{2,1,0:T(1,128)S(1)}, f32[1,1,512]{2,1,0:T(1,128)}, u32[]{:S(2)}) copy-start(f32[1,1,512]{2,1,0:T(1,128)} %get-tuple-element.147) | copy-start | bytes 6148
  117.6 5.0 %copy-start.12 = (f32[1,1,512]{2,1,0:T(1,128)S(1)}, f32[1,1,512]{2,1,0:T(1,128)}, u32[]{:S(2)}) copy-start(f32[1,1,512]{2,1,0:T(1,128)} %get-tuple-element.152) | copy-start | bytes 6148
  117.6 5.0 %copy-start.14 = (f32[1,1,512]{2,1,0:T(1,128)S(1)}, f32[1,1,512]{2,1,0:T(1,128)}, u32[]{:S(2)}) copy-start(f32[1,1,512]{2,1,0:T(1,128)} %get-tuple-element.146) | copy-start | bytes 6148
  117.6 5.0 %copy-start.16 = (f32[1,1,512]{2,1,0:T(1,128)S(1)}, f32[1,1,512]{2,1,0:T(1,128)}, u32[]{:S(2)}) copy-start(f32[1,1,512]{2,1,0:T(1,128)} %get-tuple-element.145) | copy-start | bytes 6148
  117.6 5.0 %copy-start.18 = (f32[1,1,512]{2,1,0:T(1,128)S(1)}, f32[1,1,512]{2,1,0:T(1,128)}, u32[]{:S(2)}) copy-start(f32[1,1,512]{2,1,0:T(1,128)} %get-tuple-element.144) | copy-start | bytes 6148
  117.6 5.0 %copy-start.20 = (f32[1,1,512]{2,1,0:T(1,128)S(1)}, f32[1,1,512]{2,1,0:T(1,128)}, u32[]{:S(2)}) copy-start(f32[1,1,512]{2,1,0:T(1,128)} %get-tuple-element.143) | copy-start | bytes 6148
  117.6 5.0 %copy-start.22 = (f32[1,1,512]{2,1,0:T(1,128)S(1)}, f32[1,1,512]{2,1,0:T(1,128)}, u32[]{:S(2)}) copy-start(f32[1,1,512]{2,1,0:T(1,128)} %get-tuple-element.142) | copy-start | bytes 6148
  117.6 5.0 %copy-start.23 = (f32[1,1,512]{2,1,0:T(1,128)S(1)}, f32[1,1,512]{2,1,0:T(1,128)}, u32[]{:S(2)}) copy-start(f32[1,1,512]{2,1,0:T(1,128)} %get-tuple-element.151) | copy-start | bytes 6148
  121.0 1.8 copy-start.27
  121.1 1.8 copy-start.29
  121.1 2.2 copy-start.30
  121.1 2.2 copy-start.31
  121.1 2.2 copy-start.32
  121.1 2.2 copy-start.33
  121.1 2.2 copy-start.34
  121.1 2.2 copy-start.35
  121.1 2.2 copy-start.36
  121.1 2.2 copy-start.37
  121.1 2.2 copy-start.38
  123.4 1.1 copy-start.28
  126.5 2.5 copy-start.25
  181.8 5.7 %copy-start.3 = (f32[9,9,128]{2,1,0:T(8,128)S(1)}, f32[9,9,128]{2,1,0:T(8,128)}, u32[]{:S(2)}) copy-start(f32[9,9,128]{2,1,0:T(8,128)} %param.10) | copy-start | bytes 124420
  183.2 20.8 %all-to-all-start.4 = ((bf16[16,2,9,1024]{3,1,2,0:T(2,128)(2,1)}), bf16[16,2,9,1024]{3,1,2,0:T(2,128)(2,1)S(1)}, u32[]{:S(2)}, u32[]{:S(2)}) async-start(bf16[16,2,9,1024]{3,1,2,0:T(2,128)(2,1)} %copy.312), calls=%async_computation.4 | async-start | bytes 1179648 | tf_op jit(solution)/shard_map/all_to_all | solution.py:128
  315.4 87.0 %copy-start = (f32[32,9,128]{2,0,1:T(8,128)}, f32[32,9,128]{2,0,1:T(8,128)S(1)}, u32[]{:S(2)}) copy-start(f32[32,9,128]{2,0,1:T(8,128)S(1)} %copy.323) | copy-start | bytes 442372
